TPU v7x, 32 devices: a whole 2x2x4 slice. The times are simulated.
32 devices in a mesh: cp: 32 (over z, y, x, core).
Axes of the slice: x: 2, y: 2, z: 4, core: 2. Of those that a mesh axis runs over, the one named last changes fastest.
Arguments:
- x_in_a: bfloat16 [1, 4096, 1024], P(None, 'cp')
- x_in_b: bfloat16 [1, 4096, 1024], P(None, 'cp')
- dy_out_a: bfloat16 [1, 4096, 1024], P(None, 'cp')
- dy_out_b: bfloat16 [1, 4096, 1024], P(None, 'cp')
- gain_in_a: bfloat16 [1024], replicated
- gain_in_b: bfloat16 [1024], replicated
- w_qa: bfloat16 [1024, 2048], replicated
- w_qb: bfloat16 [1024, 2048], replicated
- w_k: bfloat16 [1024, 1024], replicated
- w_v: bfloat16 [1024, 1024], replicated
- w_oa: bfloat16 [2048, 1024], replicated
- w_ob: bfloat16 [2048, 1024], replicated
- gain_qa: bfloat16 [128], replicated
- gain_qb: bfloat16 [128], replicated
- gain_k: bfloat16 [128], replicated
Outputs:
- output 1: bfloat16 [1, 4096, 1024], P(None, 'cp')
- output 2: bfloat16 [1, 4096, 1024], P(None, 'cp')
- output 3: bfloat16 [1, 4096, 1024], P(None, 'cp')
- output 4: bfloat16 [1, 4096, 1024], P(None, 'cp')
- output 5: float32 [1024, 2048], replicated
- output 6: float32 [1024, 2048], replicated
- output 7: float32 [1024, 1024], replicated
- output 8: float32 [1024, 1024], replicated
- output 9: float32 [2048, 1024], replicated
- output 10: float32 [2048, 1024], replicated
All inputs are finite; a program needn't handle non-finite values.
Results may differ from a plain program's by a relative error of at most 0.0139066.
Values are sent between devices in bfloat16 or wider.
A program may use at most 1 GiB of HBM per device.

v0:
```python
import functools
import jax
import jax.numpy as jnp
from jax import lax
from jax.sharding import PartitionSpec as P

EPSILON = 1e-6
ROPE_BASE = 10000.0
NEG_BIG = -1e30


def rms_norm(values, gain_vec):
    vals32 = values.astype(jnp.float32)
    inv_rms = lax.rsqrt(jnp.mean(vals32 * vals32, axis=-1, keepdims=True) + EPSILON)
    return vals32 * inv_rms * gain_vec.astype(jnp.float32)


def rotary(values, positions):
    half_dim = values.shape[-1] // 2
    inv_freq = ROPE_BASE ** (-jnp.arange(half_dim, dtype=jnp.float32) / half_dim)
    angles = positions.astype(jnp.float32)[:, None] * inv_freq[None, :]
    bshape = (1, positions.shape[0]) + (1,) * (values.ndim - 3) + (half_dim,)
    cos_vals = jnp.cos(angles).reshape(bshape)
    sine_vals = jnp.sin(angles).reshape(bshape)
    first_half = values[..., :half_dim]
    second_half = values[..., half_dim:]
    return jnp.concatenate([first_half * cos_vals - second_half * sine_vals, second_half * cos_vals + first_half * sine_vals], axis=-1)


def head_prep(proj_vals, gain_vec, positions):
    return rotary(rms_norm(proj_vals, gain_vec), positions)


def piece_positions(owner_dev, tok_dev, cp_size):
    piece_len = tok_dev // 2
    row_idx = jnp.arange(tok_dev)
    return jnp.where(row_idx < piece_len, owner_dev * piece_len + row_idx, (2 * cp_size - 1 - owner_dev) * piece_len + row_idx - piece_len)


def solution(mesh):
    cp_size = mesh.shape['cp']
    shift_perm = [(sender, (sender + 1) % cp_size) for sender in range(cp_size)]
    act_spec = P(None, 'cp', None)
    rep_spec = P()

    def local_fn(x_in_a, x_in_b, dy_out_a, dy_out_b, gain_in_a, gain_in_b, w_qa, w_qb, w_k, w_v, w_oa, w_ob, gain_qa, gain_qb, gain_k):
        n_batch, tok_dev = x_in_a.shape[:2]
        head_dim = gain_k.shape[0]
        kv_heads = w_k.shape[1] // head_dim
        q_width = w_qa.shape[1]
        groups = q_width // (head_dim * kv_heads)
        score_scale = head_dim ** -0.5
        my_rank = lax.axis_index('cp')
        q_pos = piece_positions(my_rank, tok_dev, cp_size)
        q_shape = (n_batch, tok_dev, kv_heads, groups, head_dim)
        kv_shape = (n_batch, tok_dev, kv_heads, head_dim)

        normed_a = rms_norm(x_in_a, gain_in_a).astype(jnp.bfloat16)
        normed_b = rms_norm(x_in_b, gain_in_b).astype(jnp.bfloat16)
        proj_qa = jnp.einsum('btd,de->bte', normed_a, w_qa, preferred_element_type=jnp.float32).reshape(q_shape)
        proj_qb = jnp.einsum('btd,de->bte', normed_b, w_qb, preferred_element_type=jnp.float32).reshape(q_shape)
        proj_k = jnp.einsum('btd,de->bte', normed_a, w_k, preferred_element_type=jnp.float32).reshape(kv_shape)
        prep_qa, pull_qa = jax.vjp(functools.partial(head_prep, gain_vec=gain_qa, positions=q_pos), proj_qa)
        prep_qb, pull_qb = jax.vjp(functools.partial(head_prep, gain_vec=gain_qb, positions=q_pos), proj_qb)
        prep_k, pull_k = jax.vjp(functools.partial(head_prep, gain_vec=gain_k, positions=q_pos), proj_k)
        queries = jnp.concatenate([prep_qa, prep_qb], axis=3).astype(jnp.bfloat16)
        keys_loc = prep_k.astype(jnp.bfloat16)
        vals_loc = jnp.einsum('btd,de->bte', normed_a, w_v, preferred_element_type=jnp.float32).astype(jnp.bfloat16).reshape(kv_shape)

        def block_scores(key_blk, sender):
            k_pos = piece_positions(sender, tok_dev, cp_size)
            causal_mask = k_pos[None, :] <= q_pos[:, None]
            scores = jnp.einsum('bqhgd,bkhd->bhgqk', queries, key_blk, preferred_element_type=jnp.float32) * score_scale
            return jnp.where(causal_mask, scores, NEG_BIG), causal_mask

        def fwd_update(run_stats, key_blk, val_blk, sender):
            run_max, run_sum, acc_out = run_stats
            masked, causal_mask = block_scores(key_blk, sender)
            new_max = jnp.maximum(run_max, jnp.max(masked, axis=-1))
            weights = jnp.where(causal_mask, jnp.exp(masked - new_max[..., None]), 0.0)
            factor = jnp.exp(run_max - new_max)
            new_sum = run_sum * factor + jnp.sum(weights, axis=-1)
            new_acc = acc_out * factor[..., None] + jnp.einsum('bhgqk,bkhd->bhgqd', weights.astype(jnp.bfloat16), val_blk, preferred_element_type=jnp.float32)
            return new_max, new_sum, new_acc

        stat_shape = (n_batch, kv_heads, 2 * groups, tok_dev)
        init_stats = (jnp.full(stat_shape, NEG_BIG, jnp.float32), jnp.zeros(stat_shape, jnp.float32), jnp.zeros(stat_shape + (head_dim,), jnp.float32))

        def fwd_body(step_idx, loop_state):
            run_stats, key_blk, val_blk = loop_state
            run_stats = fwd_update(run_stats, key_blk, val_blk, (my_rank - step_idx) % cp_size)
            key_blk, val_blk = lax.ppermute((key_blk, val_blk), 'cp', shift_perm)
            return run_stats, key_blk, val_blk

        run_stats, key_last, val_last = lax.fori_loop(0, cp_size - 1, fwd_body, (init_stats, keys_loc, vals_loc))
        run_max, run_sum, acc_out = fwd_update(run_stats, key_last, val_last, (my_rank + 1) % cp_size)
        log_norm = run_max + jnp.log(run_sum)
        attn_out = jnp.transpose(acc_out / run_sum[..., None], (0, 3, 1, 2, 4)).astype(jnp.bfloat16)
        out_a = attn_out[:, :, :, :groups, :].reshape(n_batch, tok_dev, q_width)
        out_b = attn_out[:, :, :, groups:, :].reshape(n_batch, tok_dev, q_width)
        y_out_a = (x_in_a.astype(jnp.float32) + jnp.einsum('bte,ed->btd', out_a, w_oa, preferred_element_type=jnp.float32)).astype(jnp.bfloat16)
        y_out_b = (x_in_b.astype(jnp.float32) + jnp.einsum('bte,ed->btd', out_b, w_ob, preferred_element_type=jnp.float32)).astype(jnp.bfloat16)

        d_out = jnp.concatenate([
            jnp.einsum('btd,ed->bte', dy_out_a, w_oa, preferred_element_type=jnp.float32).astype(jnp.bfloat16).reshape(q_shape),
            jnp.einsum('btd,ed->bte', dy_out_b, w_ob, preferred_element_type=jnp.float32).astype(jnp.bfloat16).reshape(q_shape)], axis=3)
        row_delta = jnp.einsum('bqhgd,bqhgd->bhgq', d_out, attn_out, preferred_element_type=jnp.float32)

        def bwd_update(dq_acc, key_blk, val_blk, dk_blk, dv_blk, sender):
            masked, causal_mask = block_scores(key_blk, sender)
            weights = jnp.where(causal_mask, jnp.exp(masked - log_norm[..., None]), 0.0)
            d_weights = jnp.einsum('bqhgd,bkhd->bhgqk', d_out, val_blk, preferred_element_type=jnp.float32)
            d_scores = (weights * (d_weights - row_delta[..., None]) * score_scale).astype(jnp.bfloat16)
            dv_blk = dv_blk + jnp.einsum('bhgqk,bqhgd->bkhd', weights.astype(jnp.bfloat16), d_out, preferred_element_type=jnp.float32)
            dk_blk = dk_blk + jnp.einsum('bhgqk,bqhgd->bkhd', d_scores, queries, preferred_element_type=jnp.float32)
            dq_acc = dq_acc + jnp.einsum('bhgqk,bkhd->bqhgd', d_scores, key_blk, preferred_element_type=jnp.float32)
            return dq_acc, dk_blk, dv_blk

        def bwd_body(step_idx, loop_state):
            dq_acc, key_blk, val_blk, dk_blk, dv_blk = loop_state
            dq_acc, dk_blk, dv_blk = bwd_update(dq_acc, key_blk, val_blk, dk_blk, dv_blk, (my_rank - step_idx) % cp_size)
            key_blk, val_blk, dk_blk, dv_blk = lax.ppermute((key_blk, val_blk, dk_blk, dv_blk), 'cp', shift_perm)
            return dq_acc, key_blk, val_blk, dk_blk, dv_blk

        kv_zero = jnp.zeros(kv_shape, jnp.float32)
        dq_acc, key_last, val_last, dk_blk, dv_blk = lax.fori_loop(0, cp_size - 1, bwd_body, (jnp.zeros(queries.shape, jnp.float32), keys_loc, vals_loc, kv_zero, kv_zero))
        dq_acc, dk_blk, dv_blk = bwd_update(dq_acc, key_last, val_last, dk_blk, dv_blk, (my_rank + 1) % cp_size)
        dk_home, dv_home = lax.ppermute((dk_blk, dv_blk), 'cp', shift_perm)

        d_proj_qa = pull_qa(dq_acc[:, :, :, :groups, :])[0].reshape(n_batch, tok_dev, q_width).astype(jnp.bfloat16)
        d_proj_qb = pull_qb(dq_acc[:, :, :, groups:, :])[0].reshape(n_batch, tok_dev, q_width).astype(jnp.bfloat16)
        d_proj_k = pull_k(dk_home)[0].reshape(n_batch, tok_dev, -1).astype(jnp.bfloat16)
        d_vals = dv_home.reshape(n_batch, tok_dev, -1).astype(jnp.bfloat16)
        dw_qa = jnp.einsum('btd,bte->de', normed_a, d_proj_qa, preferred_element_type=jnp.float32)
        dw_qb = jnp.einsum('btd,bte->de', normed_b, d_proj_qb, preferred_element_type=jnp.float32)
        dw_k = jnp.einsum('btd,bte->de', normed_a, d_proj_k, preferred_element_type=jnp.float32)
        dw_v = jnp.einsum('btd,bte->de', normed_a, d_vals, preferred_element_type=jnp.float32)
        dw_oa = jnp.einsum('bte,btd->ed', out_a, dy_out_a, preferred_element_type=jnp.float32)
        dw_ob = jnp.einsum('bte,btd->ed', out_b, dy_out_b, preferred_element_type=jnp.float32)
        d_norm_a = (jnp.einsum('bte,de->btd', d_proj_qa, w_qa, preferred_element_type=jnp.float32)
                    + jnp.einsum('bte,de->btd', d_proj_k, w_k, preferred_element_type=jnp.float32)
                    + jnp.einsum('bte,de->btd', d_vals, w_v, preferred_element_type=jnp.float32))
        d_norm_b = jnp.einsum('bte,de->btd', d_proj_qb, w_qb, preferred_element_type=jnp.float32)
        pull_na = jax.vjp(functools.partial(rms_norm, gain_vec=gain_in_a), x_in_a.astype(jnp.float32))[1]
        pull_nb = jax.vjp(functools.partial(rms_norm, gain_vec=gain_in_b), x_in_b.astype(jnp.float32))[1]
        dx_in_a = (dy_out_a.astype(jnp.float32) + pull_na(d_norm_a)[0]).astype(jnp.bfloat16)
        dx_in_b = (dy_out_b.astype(jnp.float32) + pull_nb(d_norm_b)[0]).astype(jnp.bfloat16)
        weight_grads = lax.psum((dw_qa, dw_qb, dw_k, dw_v, dw_oa, dw_ob), 'cp')
        return (y_out_a, y_out_b, dx_in_a, dx_in_b) + tuple(weight_grads)

    return jax.shard_map(local_fn, mesh=mesh, in_specs=(act_spec,) * 4 + (rep_spec,) * 11, out_specs=(act_spec,) * 4 + (rep_spec,) * 6, check_vma=False)
```

profile of v0, /device:TPU:0, one launch (start us, length us, event | category | flops | bytes accessed | tf_op | source)
XLA Modules:
  0.0 2206.7 jit_solution(6425352290148783565)
XLA Ops:
  70.4 15.0 copy.229
  90.8 381.8 %while.48 = (s32[]{:T(128)}, f32[1,8,4,128]{3,2,1,0:T(4,128)S(1)}, f32[1,8,4,128]{3,2,1,0:T(4,128)}, f32[1,8,4,128,128]{4,3,2,1,0:T(8,128)}, bf16[1,128,8,128]{3...) while((s32[]{:T(128)}, f32[1,8,4,128]{3,2,1,0:T(4,128)S(1)}, ...), condition=%wide.region_8.9_spmd.clone, body=%wide.region_5.8_spmd.clone.sunk | while | flops 276866304 | bytes 32442892 | solution.py:95
  483.3 1029.1 %while.49 = (s32[]{:T(128)}, f32[1,128,8,4,128]{4,1,3,2,0:T(8,128)}, bf16[1,128,8,128]{3,1,2,0:T(8,128)(2,1)}, bf16[1,128,8,128]{3,1,2,0:T(8,128)(2,1)}, f32[1,1...) while((s32[]{:T(128)}, ...), condition=%wide.region_12.13_spmd.clone, body=%wide.region_11.12_spmd.clone.sunk | while | flops 677135616 | bytes 28117508 | solution.py:126
  498.5 15.2 collective-permute-done.3
  532.4 14.5 collective-permute-done.3
  565.6 14.5 collective-permute-done.3
  598.8 14.5 collective-permute-done.3
  632.0 14.5 collective-permute-done.3
  665.2 14.5 collective-permute-done.3
  698.4 14.5 collective-permute-done.3
  731.6 14.5 collective-permute-done.3
  764.8 14.5 collective-permute-done.3
  798.0 14.5 collective-permute-done.3
  831.2 14.5 collective-permute-done.3
  864.4 14.5 collective-permute-done.3
  897.6 14.5 collective-permute-done.3
  930.8 14.5 collective-permute-done.3
  964.0 14.5 collective-permute-done.3
  997.2 14.5 collective-permute-done.3
  1030.4 14.5 collective-permute-done.3
  1063.6 14.5 collective-permute-done.3
  1096.8 14.5 collective-permute-done.3
  1130.0 14.5 collective-permute-done.3
  1581.7 588.8 %all-reduce.9.cloned.1.call-done = (f32[1024,2048]{1,0:T(8,128)}, f32[1024,2048]{1,0:T(8,128)}, f32[1024,1024]{1,0:T(8,128)}, f32[1024,1024]{1,0:T(8,128)}, f32[2048,1024]{1,0:T(8,128)}, /*index=5*/f32[2048,1024]{1,0:T(8,128)}) async-done(((f32[1024,2048]{1,0:T(8,128)}, f32[1024,2048]{1,0:T(8,128)}, f32[1024,1024]{1,0:T(8,128)}, f32[1024,1024]{1,0:T(8,128)}, f32[2048,1024]{1,0:T(8,128)}, ...) | async-done | bytes 41943056 | tf_op jit(solution)/shard_map/psum | solution.py:148
  (1527 shorter events, 1291.1 us)
Async XLA Ops:
  7.2 2163.3 %all-reduce.9.cloned.1.call-start = ((), (), s32[]{:S(2)}) async-start(), calls=%async_computation | async-start | bytes 83886080 | tf_op jit(solution)/shard_map/psum | solution.py:148
  493.1 23.4 %collective-permute-start.4 = (f32[1,128,8,128]{3,1,2,0:T(8,128)}, f32[1,128,8,128]{3,1,2,0:T(8,128)}, u32[]{:S(2)}, u32[]{:S(2)}) collective-permute-start(f32[1,128,8,128]{3,1,2,0:T(8,128)} %fusion.197), channel_id=1, source_target_pairs={{0,1},{1,2},{2,3},{3,4},{4,5},{5,6},{6,7},{7,8},{8,9},{9,10},{10,1... | collective-permute-start | bytes 1572872 | tf_op jit(solution)/shard_map/while/body/eval_jaxpr/ppermute | solution.py:122
  559.5 23.4 %collective-permute-start.4 = (f32[1,128,8,128]{3,1,2,0:T(8,128)}, f32[1,128,8,128]{3,1,2,0:T(8,128)}, u32[]{:S(2)}, u32[]{:S(2)}) collective-permute-start(f32[1,128,8,128]{3,1,2,0:T(8,128)} %fusion.197), channel_id=1, source_target_pairs={{0,1},{1,2},{2,3},{3,4},{4,5},{5,6},{6,7},{7,8},{8,9},{9,10},{10,1... | collective-permute-start | bytes 1572872 | tf_op jit(solution)/shard_map/while/body/eval_jaxpr/ppermute | solution.py:122
  625.9 23.4 %collective-permute-start.4 = (f32[1,128,8,128]{3,1,2,0:T(8,128)}, f32[1,128,8,128]{3,1,2,0:T(8,128)}, u32[]{:S(2)}, u32[]{:S(2)}) collective-permute-start(f32[1,128,8,128]{3,1,2,0:T(8,128)} %fusion.197), channel_id=1, source_target_pairs={{0,1},{1,2},{2,3},{3,4},{4,5},{5,6},{6,7},{7,8},{8,9},{9,10},{10,1... | collective-permute-start | bytes 1572872 | tf_op jit(solution)/shard_map/while/body/eval_jaxpr/ppermute | solution.py:122
  659.1 23.4 %collective-permute-start.4 = (f32[1,128,8,128]{3,1,2,0:T(8,128)}, f32[1,128,8,128]{3,1,2,0:T(8,128)}, u32[]{:S(2)}, u32[]{:S(2)}) collective-permute-start(f32[1,128,8,128]{3,1,2,0:T(8,128)} %fusion.197), channel_id=1, source_target_pairs={{0,1},{1,2},{2,3},{3,4},{4,5},{5,6},{6,7},{7,8},{8,9},{9,10},{10,1... | collective-permute-start | bytes 1572872 | tf_op jit(solution)/shard_map/while/body/eval_jaxpr/ppermute | solution.py:122
  692.3 23.4 %collective-permute-start.4 = (f32[1,128,8,128]{3,1,2,0:T(8,128)}, f32[1,128,8,128]{3,1,2,0:T(8,128)}, u32[]{:S(2)}, u32[]{:S(2)}) collective-permute-start(f32[1,128,8,128]{3,1,2,0:T(8,128)} %fusion.197), channel_id=1, source_target_pairs={{0,1},{1,2},{2,3},{3,4},{4,5},{5,6},{6,7},{7,8},{8,9},{9,10},{10,1... | collective-permute-start | bytes 1572872 | tf_op jit(solution)/shard_map/while/body/eval_jaxpr/ppermute | solution.py:122
  725.5 23.4 %collective-permute-start.4 = (f32[1,128,8,128]{3,1,2,0:T(8,128)}, f32[1,128,8,128]{3,1,2,0:T(8,128)}, u32[]{:S(2)}, u32[]{:S(2)}) collective-permute-start(f32[1,128,8,128]{3,1,2,0:T(8,128)} %fusion.197), channel_id=1, source_target_pairs={{0,1},{1,2},{2,3},{3,4},{4,5},{5,6},{6,7},{7,8},{8,9},{9,10},{10,1... | collective-permute-start | bytes 1572872 | tf_op jit(solution)/shard_map/while/body/eval_jaxpr/ppermute | solution.py:122
  758.7 23.4 %collective-permute-start.4 = (f32[1,128,8,128]{3,1,2,0:T(8,128)}, f32[1,128,8,128]{3,1,2,0:T(8,128)}, u32[]{:S(2)}, u32[]{:S(2)}) collective-permute-start(f32[1,128,8,128]{3,1,2,0:T(8,128)} %fusion.197), channel_id=1, source_target_pairs={{0,1},{1,2},{2,3},{3,4},{4,5},{5,6},{6,7},{7,8},{8,9},{9,10},{10,1... | collective-permute-start | bytes 1572872 | tf_op jit(solution)/shard_map/while/body/eval_jaxpr/ppermute | solution.py:122
  791.8 23.4 %collective-permute-start.4 = (f32[1,128,8,128]{3,1,2,0:T(8,128)}, f32[1,128,8,128]{3,1,2,0:T(8,128)}, u32[]{:S(2)}, u32[]{:S(2)}) collective-permute-start(f32[1,128,8,128]{3,1,2,0:T(8,128)} %fusion.197), channel_id=1, source_target_pairs={{0,1},{1,2},{2,3},{3,4},{4,5},{5,6},{6,7},{7,8},{8,9},{9,10},{10,1... | collective-permute-start | bytes 1572872 | tf_op jit(solution)/shard_map/while/body/eval_jaxpr/ppermute | solution.py:122
  858.2 23.4 %collective-permute-start.4 = (f32[1,128,8,128]{3,1,2,0:T(8,128)}, f32[1,128,8,128]{3,1,2,0:T(8,128)}, u32[]{:S(2)}, u32[]{:S(2)}) collective-permute-start(f32[1,128,8,128]{3,1,2,0:T(8,128)} %fusion.197), channel_id=1, source_target_pairs={{0,1},{1,2},{2,3},{3,4},{4,5},{5,6},{6,7},{7,8},{8,9},{9,10},{10,1... | collective-permute-start | bytes 1572872 | tf_op jit(solution)/shard_map/while/body/eval_jaxpr/ppermute | solution.py:122
  924.6 23.4 %collective-permute-start.4 = (f32[1,128,8,128]{3,1,2,0:T(8,128)}, f32[1,128,8,128]{3,1,2,0:T(8,128)}, u32[]{:S(2)}, u32[]{:S(2)}) collective-permute-start(f32[1,128,8,128]{3,1,2,0:T(8,128)} %fusion.197), channel_id=1, source_target_pairs={{0,1},{1,2},{2,3},{3,4},{4,5},{5,6},{6,7},{7,8},{8,9},{9,10},{10,1... | collective-permute-start | bytes 1572872 | tf_op jit(solution)/shard_map/while/body/eval_jaxpr/ppermute | solution.py:122
  991.0 23.4 %collective-permute-start.4 = (f32[1,128,8,128]{3,1,2,0:T(8,128)}, f32[1,128,8,128]{3,1,2,0:T(8,128)}, u32[]{:S(2)}, u32[]{:S(2)}) collective-permute-start(f32[1,128,8,128]{3,1,2,0:T(8,128)} %fusion.197), channel_id=1, source_target_pairs={{0,1},{1,2},{2,3},{3,4},{4,5},{5,6},{6,7},{7,8},{8,9},{9,10},{10,1... | collective-permute-start | bytes 1572872 | tf_op jit(solution)/shard_map/while/body/eval_jaxpr/ppermute | solution.py:122
  1057.4 23.4 %collective-permute-start.4 = (f32[1,128,8,128]{3,1,2,0:T(8,128)}, f32[1,128,8,128]{3,1,2,0:T(8,128)}, u32[]{:S(2)}, u32[]{:S(2)}) collective-permute-start(f32[1,128,8,128]{3,1,2,0:T(8,128)} %fusion.197), channel_id=1, source_target_pairs={{0,1},{1,2},{2,3},{3,4},{4,5},{5,6},{6,7},{7,8},{8,9},{9,10},{10,1... | collective-permute-start | bytes 1572872 | tf_op jit(solution)/shard_map/while/body/eval_jaxpr/ppermute | solution.py:122
  1123.8 23.4 %collective-permute-start.4 = (f32[1,128,8,128]{3,1,2,0:T(8,128)}, f32[1,128,8,128]{3,1,2,0:T(8,128)}, u32[]{:S(2)}, u32[]{:S(2)}) collective-permute-start(f32[1,128,8,128]{3,1,2,0:T(8,128)} %fusion.197), channel_id=1, source_target_pairs={{0,1},{1,2},{2,3},{3,4},{4,5},{5,6},{6,7},{7,8},{8,9},{9,10},{10,1... | collective-permute-start | bytes 1572872 | tf_op jit(solution)/shard_map/while/body/eval_jaxpr/ppermute | solution.py:122
  1190.2 23.4 %collective-permute-start.4 = (f32[1,128,8,128]{3,1,2,0:T(8,128)}, f32[1,128,8,128]{3,1,2,0:T(8,128)}, u32[]{:S(2)}, u32[]{:S(2)}) collective-permute-start(f32[1,128,8,128]{3,1,2,0:T(8,128)} %fusion.197), channel_id=1, source_target_pairs={{0,1},{1,2},{2,3},{3,4},{4,5},{5,6},{6,7},{7,8},{8,9},{9,10},{10,1... | collective-permute-start | bytes 1572872 | tf_op jit(solution)/shard_map/while/body/eval_jaxpr/ppermute | solution.py:122
  1256.6 23.4 %collective-permute-start.4 = (f32[1,128,8,128]{3,1,2,0:T(8,128)}, f32[1,128,8,128]{3,1,2,0:T(8,128)}, u32[]{:S(2)}, u32[]{:S(2)}) collective-permute-start(f32[1,128,8,128]{3,1,2,0:T(8,128)} %fusion.197), channel_id=1, source_target_pairs={{0,1},{1,2},{2,3},{3,4},{4,5},{5,6},{6,7},{7,8},{8,9},{9,10},{10,1... | collective-permute-start | bytes 1572872 | tf_op jit(solution)/shard_map/while/body/eval_jaxpr/ppermute | solution.py:122
  1289.8 23.4 %collective-permute-start.4 = (f32[1,128,8,128]{3,1,2,0:T(8,128)}, f32[1,128,8,128]{3,1,2,0:T(8,128)}, u32[]{:S(2)}, u32[]{:S(2)}) collective-permute-start(f32[1,128,8,128]{3,1,2,0:T(8,128)} %fusion.197), channel_id=1, source_target_pairs={{0,1},{1,2},{2,3},{3,4},{4,5},{5,6},{6,7},{7,8},{8,9},{9,10},{10,1... | collective-permute-start | bytes 1572872 | tf_op jit(solution)/shard_map/while/body/eval_jaxpr/ppermute | solution.py:122
  1323.0 23.4 %collective-permute-start.4 = (f32[1,128,8,128]{3,1,2,0:T(8,128)}, f32[1,128,8,128]{3,1,2,0:T(8,128)}, u32[]{:S(2)}, u32[]{:S(2)}) collective-permute-start(f32[1,128,8,128]{3,1,2,0:T(8,128)} %fusion.197), channel_id=1, source_target_pairs={{0,1},{1,2},{2,3},{3,4},{4,5},{5,6},{6,7},{7,8},{8,9},{9,10},{10,1... | collective-permute-start | bytes 1572872 | tf_op jit(solution)/shard_map/while/body/eval_jaxpr/ppermute | solution.py:122
  1356.2 23.4 %collective-permute-start.4 = (f32[1,128,8,128]{3,1,2,0:T(8,128)}, f32[1,128,8,128]{3,1,2,0:T(8,128)}, u32[]{:S(2)}, u32[]{:S(2)}) collective-permute-start(f32[1,128,8,128]{3,1,2,0:T(8,128)} %fusion.197), channel_id=1, source_target_pairs={{0,1},{1,2},{2,3},{3,4},{4,5},{5,6},{6,7},{7,8},{8,9},{9,10},{10,1... | collective-permute-start | bytes 1572872 | tf_op jit(solution)/shard_map/while/body/eval_jaxpr/ppermute | solution.py:122
  1389.4 23.4 %collective-permute-start.4 = (f32[1,128,8,128]{3,1,2,0:T(8,128)}, f32[1,128,8,128]{3,1,2,0:T(8,128)}, u32[]{:S(2)}, u32[]{:S(2)}) collective-permute-start(f32[1,128,8,128]{3,1,2,0:T(8,128)} %fusion.197), channel_id=1, source_target_pairs={{0,1},{1,2},{2,3},{3,4},{4,5},{5,6},{6,7},{7,8},{8,9},{9,10},{10,1... | collective-permute-start | bytes 1572872 | tf_op jit(solution)/shard_map/while/body/eval_jaxpr/ppermute | solution.py:122
  1422.6 23.4 %collective-permute-start.4 = (f32[1,128,8,128]{3,1,2,0:T(8,128)}, f32[1,128,8,128]{3,1,2,0:T(8,128)}, u32[]{:S(2)}, u32[]{:S(2)}) collective-permute-start(f32[1,128,8,128]{3,1,2,0:T(8,128)} %fusion.197), channel_id=1, source_target_pairs={{0,1},{1,2},{2,3},{3,4},{4,5},{5,6},{6,7},{7,8},{8,9},{9,10},{10,1... | collective-permute-start | bytes 1572872 | tf_op jit(solution)/shard_map/while/body/eval_jaxpr/ppermute | solution.py:122
  1489.0 23.4 %collective-permute-start.4 = (f32[1,128,8,128]{3,1,2,0:T(8,128)}, f32[1,128,8,128]{3,1,2,0:T(8,128)}, u32[]{:S(2)}, u32[]{:S(2)}) collective-permute-start(f32[1,128,8,128]{3,1,2,0:T(8,128)} %fusion.197), channel_id=1, source_target_pairs={{0,1},{1,2},{2,3},{3,4},{4,5},{5,6},{6,7},{7,8},{8,9},{9,10},{10,1... | collective-permute-start | bytes 1572872 | tf_op jit(solution)/shard_map/while/body/eval_jaxpr/ppermute | solution.py:122
  1519.4 39.0 %collective-permute-start.7 = (bf16[1,128,8,128]{1,3,2,0:T(8,128)(2,1)}, bf16[1,128,8,128]{1,3,2,0:T(8,128)(2,1)}, u32[]{:S(2)}, u32[]{:S(2)}) collective-permute-start(bf16[1,128,8,128]{1,3,2,0:T(8,128)(2,1)} %fusion.53), channel_id=1, source_target_pairs={{0,1},{1,2},{2,3},{3,4},{4,5},{5,6},{6,7},{7,8},{8,9},{9,10},{10,1... | collective-permute-start | bytes 786440 | tf_op jit(solution)/shard_map/ppermute | solution.py:128
  1524.5 37.7 %collective-permute-start.6 = (f32[1,128,8,128]{1,3,2,0:T(8,128)}, f32[1,128,8,128]{1,3,2,0:T(8,128)}, u32[]{:S(2)}, u32[]{:S(2)}) collective-permute-start(f32[1,128,8,128]{1,3,2,0:T(8,128)} %fusion.52), channel_id=1, source_target_pairs={{0,1},{1,2},{2,3},{3,4},{4,5},{5,6},{6,7},{7,8},{8,9},{9,10},{10,1... | collective-permute-start | bytes 1572872 | tf_op jit(solution)/shard_map/ppermute | solution.py:128
  (367 other events, 3516.3 us)
Sparse Core Ops, SparseCore 0:
  1567.4 603.0 all-reduce.8
where the time goes:
time: 2220 us; the launch traced here: 2210 us
  waiting for transfers between devices  1350 us (61%)
  matrix products  576 us (26%)
  local copies, waits for them, and re-layouts  190 us (9%)
  other arithmetic  63.1 us (3%)
    psum x1, waiting for transfers between devices, local_fn(): weight_grads = lax.psum((dw_qa, dw_qb, dw_k, dw_v, dw_oa, dw_ob), 'cp')  589 us
    ppermute x124, waiting for transfers between devices, bwd_body(): lax.ppermute((key_blk, val_blk, dk_blk, dv_blk), 'cp', shift_perm)  537 us
    ppermute x62, waiting for transfers between devices, fwd_body(): key_blk, val_blk = lax.ppermute((key_blk, val_blk), 'cp', shift_perm)  224 us
    dot_general x64, matrix products, block_scores(): jnp.einsum('bqhgd,bkhd->bhgqk', queries, key_blk, preferred_element_type=...  120 us
    dot_general x32, matrix products, bwd_update(): jnp.einsum('bhgqk,bkhd->bqhgd', d_scores, key_blk, preferred_element_type...  110 us
    while x403, local copies, waits for them, and re-layouts  106 us
    dot_general x32, matrix products, bwd_update(): jnp.einsum('bhgqk,bqhgd->bkhd', weights.astype(jnp.bfloat16), d_out, pref...  83.3 us
    dot_general x32, matrix products, bwd_update(): jnp.einsum('bhgqk,bqhgd->bkhd', d_scores, queries, preferred_element_type...  81.2 us
  transfers between devices with their start and end apart: 189, of which 125 were waited for; matrix products, arithmetic and copies ran while one was open for 18% of the time, Pallas kernels for 0%

commit v1 on v0

v1 whole, which is shorter than its diff:
```python
import functools
import jax
import jax.numpy as jnp
from jax import lax
from jax.experimental import pallas as pl
from jax.experimental.pallas import tpu as pltpu
from jax.sharding import PartitionSpec as P

EPSILON = 1e-6
ROPE_BASE = 10000.0
NEG_BIG = -1e30
LOG2E = 1.4426950408889634
F32 = jnp.float32
BF16 = jnp.bfloat16
HD, DM, SEQ, BLK, PC, HALF, ND, NB, NG = 128, 1024, 4096, 512, 64, 2048, 32, 8, 4
VMEM_LIMIT = 58 * 1024 * 1024


def rms_norm(values, gain_vec):
    vals32 = values.astype(F32)
    inv_rms = lax.rsqrt(jnp.mean(vals32 * vals32, axis=-1, keepdims=True) + EPSILON)
    return vals32 * inv_rms * gain_vec.astype(F32)


def head_norm_rope(proj, gain, cos_full, sin_full):
    inv = lax.rsqrt(jnp.mean(proj * proj, axis=-1, keepdims=True) + EPSILON)
    normed = proj * inv * gain
    return normed * cos_full + jnp.concatenate([normed[:, PC:], normed[:, :PC]], axis=-1) * sin_full


def head_norm_rope_vjp(grad, proj, gain, cos_full, sin_full):
    gs = grad * sin_full
    dn = (grad * cos_full + jnp.concatenate([gs[:, PC:], gs[:, :PC]], axis=-1)) * gain
    inv = lax.rsqrt(jnp.mean(proj * proj, axis=-1, keepdims=True) + EPSILON)
    xhat = proj * inv
    return inv * (dn - xhat * jnp.mean(dn * xhat, axis=-1, keepdims=True))


def dot(a, b, ca, cb):
    return lax.dot_general(a, b, (((ca,), (cb,)), ((), ())), preferred_element_type=F32)


def piece_row(dev, half):
    return pl.multiple_of((dev if half == 0 else 63 - dev) * PC, PC)


def proj_kernel(idx_ref, hl_ref, ha_ref, wq_ref, wkv_ref, gq_ref, gk_ref, cos_ref, sin_ref,
                q_ref, k_ref, v_ref, qp_ref, kp_ref):
    t = pl.program_id(0)
    qp = dot(hl_ref[...].reshape(BLK, DM), wq_ref[...], 1, 0)
    kvp = dot(ha_ref[...].reshape(BLK, DM), wkv_ref[...], 1, 0)
    for u in range(NG):
        for half in range(2):
            rows = slice(u * HD + half * PC, u * HD + half * PC + PC)
            dst = pl.ds(piece_row(t * NG + u, half), PC)
            cos_p, sin_p = cos_ref[dst, :], sin_ref[dst, :]
            qp_ref[dst, :] = qp[rows]
            kp_ref[dst, :] = kvp[rows, :HD]
            q_ref[dst, :] = head_norm_rope(qp[rows], gq_ref[...], cos_p, sin_p).astype(BF16)
            k_ref[dst, :] = head_norm_rope(kvp[rows, :HD], gk_ref[...], cos_p, sin_p).astype(BF16)
            v_ref[dst, :] = kvp[rows, HD:].astype(BF16)


def dout_kernel(idx_ref, dy_ref, wo_ref, do_ref):
    t = pl.program_id(0)
    d_out = dot(dy_ref[...].reshape(BLK, DM), wo_ref[...], 1, 1).astype(BF16)
    for u in range(NG):
        for half in range(2):
            rows = slice(u * HD + half * PC, u * HD + half * PC + PC)
            do_ref[pl.ds(piece_row(t * NG + u, half), PC), :] = d_out[rows]


def store_pieces(ref, block, blk_idx, count):
    for u in range(count):
        piece = blk_idx * count + u
        rows = block[u * PC:(u + 1) * PC]

        @pl.when(piece < ND)
        def _():
            ref[piece, 0:PC, :] = rows

        @pl.when(piece >= ND)
        def _():
            ref[63 - piece, PC:HD, :] = rows


def fwd_kernel(q_ref, k_ref, v_ref, o_ref, lse_ref, acc_ref, *, scale):
    i = pl.program_id(0)
    q = q_ref[...]
    c2 = scale * LOG2E

    def step(j, carry, masked):
        m, l = carry
        rows = pl.ds(pl.multiple_of(j * BLK, BLK), BLK)
        s = dot(k_ref[rows, :], q, 1, 1)
        if masked:
            kid = lax.broadcasted_iota(jnp.int32, (BLK, BLK), 0)
            qid = lax.broadcasted_iota(jnp.int32, (BLK, BLK), 1)
            s = jnp.where(kid <= qid, s, NEG_BIG)
        m_new = jnp.maximum(m, jnp.max(s, axis=0, keepdims=True))
        p = jnp.exp2((s - m_new) * c2)
        alpha = jnp.exp2((m - m_new) * c2)
        l_new = l * alpha + jnp.sum(p, axis=0, keepdims=True)
        acc_ref[...] = acc_ref[...] * alpha + dot(v_ref[rows, :], p.astype(BF16), 0, 0)
        return m_new, l_new

    acc_ref[...] = jnp.zeros_like(acc_ref)
    init = (jnp.full((1, BLK), NEG_BIG, F32), jnp.zeros((1, BLK), F32))
    m, l = step(i, init, True)
    m, l = lax.fori_loop(0, i, lambda j, cr: step(j, cr, False), (m, l))
    lse_ref[i] = m * scale + jnp.log(l)
    o_blk = (acc_ref[...] / l).T.astype(BF16)
    store_pieces(o_ref, o_blk, i, NB)


def bwd_kernel(idx_ref, q_ref, k_ref, v_ref, do_ref, o_ref, lse_ref, qp_ref, gq_ref, cos_ref, sin_ref,
               dq_ref, dkv_ref, dqt_ref, dk_acc, dv_acc, delta_ref, *, scale):
    j = pl.program_id(0)
    layer, core = idx_ref[0], idx_ref[1]
    k = k_ref[...]
    v = v_ref[...]
    c2 = scale * LOG2E

    @pl.when(j == 0)
    def _():
        dqt_ref[...] = jnp.zeros_like(dqt_ref)
        for i in range(NB):
            parts = []
            for u in range(NB):
                piece = i * NB + u
                if piece < ND:
                    parts.append(o_ref[piece, 0:PC, :])
                else:
                    parts.append(o_ref[63 - piece, PC:HD, :])
            o_blk = jnp.concatenate(parts, axis=0).astype(F32)
            prod = o_blk * do_ref[i * BLK:(i + 1) * BLK, :].astype(F32)
            delta_ref[i] = jnp.sum(prod.T, axis=0, keepdims=True)

    dk_acc[...] = jnp.zeros_like(dk_acc)
    dv_acc[...] = jnp.zeros_like(dv_acc)

    def step(i, masked):
        rows = pl.ds(pl.multiple_of(i * BLK, BLK), BLK)
        q = q_ref[rows, :]
        do = do_ref[rows, :]
        s = dot(k, q, 1, 1)
        p = jnp.exp2(s * c2 - lse_ref[i] * LOG2E)
        if masked:
            kid = lax.broadcasted_iota(jnp.int32, (BLK, BLK), 0)
            qid = lax.broadcasted_iota(jnp.int32, (BLK, BLK), 1)
            p = jnp.where(kid <= qid, p, 0.0)
        dp = dot(v, do, 1, 1)
        ds = (p * (dp - delta_ref[i]) * scale).astype(BF16)
        dv_acc[...] += dot(p.astype(BF16), do, 1, 0)
        dk_acc[...] += dot(ds, q, 1, 0)
        dqt_ref[i] += dot(k, ds, 0, 0)

    step(j, True)

    @pl.loop(j + 1, NB)
    def _(i):
        step(i, False)

    pos = jnp.where(j // NG == layer, 0, 1)
    rows = pl.ds(pl.multiple_of((j % NG) * BLK, BLK), BLK)
    dkv_ref[core, pos, rows, :] = dk_acc[...]
    dkv_ref[1 - core, pos, rows, :] = dv_acc[...]

    rows_q = pl.ds(pl.multiple_of(j * BLK, BLK), BLK)
    dq = dqt_ref[j].T
    d_proj = head_norm_rope_vjp(dq, qp_ref[rows_q, :], gq_ref[...], cos_ref[rows_q, :], sin_ref[rows_q, :])
    store_pieces(dq_ref, d_proj.astype(BF16), j, NB)


def dwo_kernel(idx_ref, o_ref, dy_ref, out_ref):
    @pl.when(pl.program_id(0) == 0)
    def _():
        out_ref[...] = jnp.zeros_like(out_ref)

    out_ref[...] += dot(o_ref[...].reshape(BLK, HD), dy_ref[...].reshape(BLK, DM), 0, 0)


def dwq_kernel(idx_ref, h_ref, d_ref, out_ref, acc_ref):
    t = pl.program_id(0)

    @pl.when(t == 0)
    def _():
        acc_ref[...] = jnp.zeros_like(acc_ref)

    acc_ref[...] += dot(d_ref[...].reshape(BLK, HD), h_ref[...].reshape(BLK, acc_ref.shape[1]), 0, 0)

    @pl.when(t == pl.num_programs(0) - 1)
    def _():
        out_ref[...] = acc_ref[...].T


def full(shape):
    return pl.BlockSpec(shape, lambda t, *_: (0,) * len(shape), pipeline_mode=pl.Buffered(1))


def full_out(shape):
    return pl.BlockSpec(shape, lambda t, *_: (0,) * len(shape))


def call(body, name, grid, in_specs, out_specs, out_shape, flops, scratch=(), prefetch=1):
    return pl.pallas_call(
        body, name=name, out_shape=out_shape,
        grid_spec=pltpu.PrefetchScalarGridSpec(
            num_scalar_prefetch=prefetch, grid=grid, in_specs=in_specs, out_specs=out_specs,
            scratch_shapes=list(scratch)),
        compiler_params=pltpu.CompilerParams(
            dimension_semantics=("arbitrary",), vmem_limit_bytes=VMEM_LIMIT),
        cost_estimate=pl.CostEstimate(flops=int(flops), bytes_accessed=1 << 23, transcendentals=0))


def solution(mesh):
    act_spec = P(None, 'cp', None)
    rep_spec = P()
    ndev = mesh.shape['cp']
    core_perm = [(s, s ^ 1) for s in range(ndev)]
    layer_perm = [(s, s ^ 2) for s in range(ndev)]

    def local_fn(x_in_a, x_in_b, dy_out_a, dy_out_b, gain_in_a, gain_in_b, w_qa, w_qb, w_k, w_v, w_oa, w_ob, gain_qa, gain_qb, gain_k):
        scale = HD ** -0.5
        rank = lax.axis_index('cp')
        grp, layer, core = rank // NG, (rank // 2) % 2, rank % 2
        head = 2 * grp + core
        is_a = layer == 0
        idx = jnp.stack([layer, core]).astype(jnp.int32)

        h_loc = jnp.stack([rms_norm(x_in_a[0], gain_in_a).astype(BF16), rms_norm(x_in_b[0], gain_in_b).astype(BF16)])
        h_all = lax.all_gather(h_loc, 'cp')
        dy_loc, h_all = lax.optimization_barrier((jnp.stack([dy_out_a[0], dy_out_b[0]]), h_all))
        dy_all = lax.all_gather(dy_loc, 'cp')

        def cols(w, at):
            return lax.dynamic_slice(w, (0, at * HD), (w.shape[0], HD))

        wq = jnp.where(is_a, cols(w_qa, head), cols(w_qb, head))
        wkv = jnp.concatenate([cols(w_k, grp), cols(w_v, grp)], axis=1)
        wo = jnp.where(is_a, lax.dynamic_slice(w_oa, (head * HD, 0), (HD, DM)),
                       lax.dynamic_slice(w_ob, (head * HD, 0), (HD, DM)))
        gq = jnp.where(is_a, gain_qa, gain_qb).astype(F32).reshape(1, HD)
        gk = gain_k.astype(F32).reshape(1, HD)
        inv_freq = ROPE_BASE ** (-jnp.arange(PC, dtype=F32) / PC)
        angles = jnp.arange(SEQ, dtype=F32)[:, None] * inv_freq[None, :]
        cos_h, sin_h = jnp.cos(angles), jnp.sin(angles)
        cos_t = jnp.concatenate([cos_h, cos_h], axis=1)
        sin_t = jnp.concatenate([-sin_h, sin_h], axis=1)

        sds = jax.ShapeDtypeStruct
        tok = (SEQ, HD)
        q, k, v, qp, kp = call(
            proj_kernel, "proj", (NB,),
            [pl.BlockSpec((NG, 1, HD, DM), lambda t, ix: (t, ix[0], 0, 0)),
             pl.BlockSpec((NG, 1, HD, DM), lambda t, ix: (t, 0, 0, 0)),
             full((DM, HD)), full((DM, 256)), full((1, HD)), full((1, HD)), full(tok), full(tok)],
            [full_out(tok)] * 5,
            [sds(tok, BF16)] * 3 + [sds(tok, F32)] * 2, 2 * SEQ * DM * 384,
        )(idx, h_all, h_all, wq, wkv, gq, gk, cos_t, sin_t)

        o, lse = call(
            functools.partial(lambda ix, *a, scale: fwd_kernel(*a, scale=scale), scale=scale), "attn_fwd", (NB,),
            [pl.BlockSpec((BLK, HD), lambda t, ix: (t, 0)), full(tok), full(tok)],
            [full_out((ND, HD, HD)), full_out((NB, 1, BLK))],
            [sds((ND, HD, HD), BF16), sds((NB, 1, BLK), F32)], NG * SEQ * SEQ * HD,
            scratch=[pltpu.VMEM((HD, BLK), F32)],
        )(idx, q, k, v)
        o_tok = lax.all_to_all(o, 'cp', 0, 0)

        do = call(
            dout_kernel, "dout", (NB,),
            [pl.BlockSpec((NG, 1, HD, DM), lambda t, ix: (t, ix[0], 0, 0)), full((HD, DM))],
            full_out(tok), sds(tok, BF16), 2 * SEQ * DM * HD,
        )(idx, dy_all, wo)
        dwo = call(
            dwo_kernel, "dwo", (NB,),
            [pl.BlockSpec((NG, HD, HD), lambda t, ix: (t, 0, 0)),
             pl.BlockSpec((NG, 1, HD, DM), lambda t, ix: (t, ix[0], 0, 0))],
            full_out((HD, DM)), sds((HD, DM), F32), 2 * SEQ * DM * HD,
        )(idx, o, dy_all)
        dwo_all = lax.all_gather(dwo, 'cp')
        do, dwo = lax.optimization_barrier((do, dwo))

        dqp, dkv = call(
            functools.partial(bwd_kernel, scale=scale), "attn_bwd", (NB,),
            [full(tok), pl.BlockSpec((BLK, HD), lambda t, ix: (t, 0)), pl.BlockSpec((BLK, HD), lambda t, ix: (t, 0)),
             full(tok), full((ND, HD, HD)), full((NB, 1, BLK)), full(tok), full((1, HD)), full(tok), full(tok)],
            [full_out((ND, HD, HD)), full_out((2, 2, HALF, HD))],
            [sds((ND, HD, HD), BF16), sds((2, 2, HALF, HD), F32)], 10 * SEQ * SEQ * HD,
            scratch=[pltpu.VMEM((NB, HD, BLK), F32), pltpu.VMEM((BLK, HD), F32), pltpu.VMEM((BLK, HD), F32),
                     pltpu.VMEM((NB, 1, BLK), F32)],
        )(idx, q, k, v, do, o, lse, qp, gq, cos_t, sin_t)

        def dw_call(name, d_st, width, col, lay):
            return call(
                dwq_kernel, name, (NB,),
                [pl.BlockSpec((NG, 1, HD, width), lambda t, ix: (t, ix[0] if lay else 0, 0, 0 if width == DM else ix[0])),
                 pl.BlockSpec((NG, HD, HD), lambda t, ix: (t, 0, 0))],
                full_out((width, HD)), sds((width, HD), F32), 2 * SEQ * width * HD,
                scratch=[pltpu.VMEM((HD, width), F32)],
            )(idx, h_all, d_st)

        dwq = dw_call("dwq", dqp, DM, 0, True)
        dwq, dwo_all = lax.optimization_barrier((dwq, dwo_all))
        dwo_all = dwo_all.reshape(NB, 2, 256, DM)
        dwq_all = lax.all_gather(dwq, 'cp').reshape(NB, 2, 2, DM, HD)

        sum1 = dkv[0] + lax.ppermute(dkv[1], 'cp', core_perm)
        tot = sum1[0] + lax.ppermute(sum1[1], 'cp', layer_perm)
        half_at = (layer * HALF, 0)
        dk_proj = head_norm_rope_vjp(tot, lax.dynamic_slice(kp, half_at, (HALF, HD)), gk,
                                     lax.dynamic_slice(cos_t, half_at, (HALF, HD)),
                                     lax.dynamic_slice(sin_t, half_at, (HALF, HD)))
        mine = jnp.where(core == 0, dk_proj, tot).astype(BF16).reshape(ND, PC, HD)
        mine = jnp.where(is_a, mine, mine[::-1])
        other = lax.ppermute(mine, 'cp', layer_perm)
        d_kv_st = jnp.concatenate([jnp.where(is_a, mine, other), jnp.where(is_a, other, mine)], axis=1)

        back = lax.all_to_all(jnp.concatenate([dqp, mine], axis=1), 'cp', 0, 0).reshape(NB, 2, 2, 192, HD)
        dwkv = dw_call("dwkv", d_kv_st, BLK, 0, False)
        dwkv_all = lax.all_gather(dwkv, 'cp').reshape(NB, 2, 2, BLK, HD)

        o_tok = o_tok.reshape(NB, 2, 2, HD, HD)
        out_a = o_tok[:, 0].transpose(2, 0, 1, 3).reshape(HD, HALF)
        out_b = o_tok[:, 1].transpose(2, 0, 1, 3).reshape(HD, HALF)
        y_out_a = (x_in_a[0].astype(F32) + dot(out_a, w_oa, 1, 0)).astype(BF16)[None]
        y_out_b = (x_in_b[0].astype(F32) + dot(out_b, w_ob, 1, 0)).astype(BF16)[None]

        d_qa = back[:, 0, :, :HD].transpose(2, 0, 1, 3).reshape(HD, HALF)
        d_qb = back[:, 1, :, :HD].transpose(2, 0, 1, 3).reshape(HD, HALF)
        d_k = back[:, :, 0, HD:].transpose(1, 2, 0, 3).reshape(HD, DM)
        d_v = back[:, :, 1, HD:].transpose(1, 2, 0, 3).reshape(HD, DM)
        d_norm_a = dot(d_qa, w_qa, 1, 1) + dot(d_k, w_k, 1, 1) + dot(d_v, w_v, 1, 1)
        d_norm_b = dot(d_qb, w_qb, 1, 1)
        pull_na = jax.vjp(functools.partial(rms_norm, gain_vec=gain_in_a), x_in_a[0].astype(F32))[1]
        pull_nb = jax.vjp(functools.partial(rms_norm, gain_vec=gain_in_b), x_in_b[0].astype(F32))[1]
        dx_in_a = (dy_out_a[0].astype(F32) + pull_na(d_norm_a)[0]).astype(BF16)[None]
        dx_in_b = (dy_out_b[0].astype(F32) + pull_nb(d_norm_b)[0]).astype(BF16)[None]

        dw_oa = dwo_all[:, 0].reshape(HALF, DM)
        dw_ob = dwo_all[:, 1].reshape(HALF, DM)
        dw_qa = dwq_all[:, 0].transpose(2, 0, 1, 3).reshape(DM, HALF)
        dw_qb = dwq_all[:, 1].transpose(2, 0, 1, 3).reshape(DM, HALF)
        dw_k = dwkv_all[:, :, 0].transpose(1, 2, 0, 3).reshape(DM, DM)
        dw_v = dwkv_all[:, :, 1].transpose(1, 2, 0, 3).reshape(DM, DM)
        return y_out_a, y_out_b, dx_in_a, dx_in_b, dw_qa, dw_qb, dw_k, dw_v, dw_oa, dw_ob

    return jax.shard_map(local_fn, mesh=mesh, in_specs=(act_spec,) * NG + (rep_spec,) * 11, out_specs=(act_spec,) * NG + (rep_spec,) * 6, check_vma=False)
```

time: 2220 us -> 696 us (0.31)
  waiting for transfers between devices: 1350 us -> 397 us
  matrix products: 576 us -> 12.5 us
  Pallas kernels: 0 us -> 122 us
  local copies, waits for them, and re-layouts: 190 us -> 98 us
  other arithmetic: 63.1 us -> 34.4 us
    ppermute x188 -> x3, waiting for transfers between devices: 761 us -> 61.4 us  [the longest x1 45.4 us: local_fn(): tot = sum1[0] + lax.ppermute(sum1[1], 'cp', layer_perm)]
    psum x1 -> x0, waiting for transfers between devices: 589 us -> none  [local_fn(): weight_grads = lax.psum((dw_qa, dw_qb, dw_k, dw_v, dw_oa, dw_ob), 'cp')]
    dot_general x242 -> x6, matrix products: 576 us -> 12.5 us  [dot(): lax.dot_general(a, b, (((ca,), (cb,)), ((), ())), preferred_element_type=...]
    all_gather x0 -> x5, waiting for transfers between devices: none -> 245 us  [the longest x1 116 us: local_fn(): h_all = lax.all_gather(h_loc, 'cp')]
    pallas_call x0 -> x7, Pallas kernels: none -> 122 us  [the longest x1 40.9 us: local_fn(): call(functools.partial(bwd_kernel, scale=scale), 'attn_bwd', (NB,), [full...]
    while x406 -> x0, local copies, waits for them, and re-layouts: 111 us -> none
    all_to_all x0 -> x2, waiting for transfers between devices: none -> 89.8 us  [the longest x1 50.2 us: local_fn(): lax.all_to_all(jnp.concatenate([dqp, mine], axis=1), 'cp', 0, 0)]
    transpose x0 -> x6, local copies, waits for them, and re-layouts: none -> 47.5 us  [the longest x2 25.4 us: local_fn(): dw_qb = dwq_all[:, 1].transpose(2, 0, 1, 3).reshape(DM, HALF)]
  transfers between devices with their start and end apart: 189 -> 10, of which waited for: 125 -> 8; matrix products, arithmetic and copies ran while one was open for 18% -> 11% of each run, Pallas kernels for 0% -> 17%
where the time goes in v1:
time: 696 us; the launch traced here: 688 us
  waiting for transfers between devices  397 us (57%)
  Pallas kernels  122 us (18%)
  local copies, waits for them, and re-layouts  98 us (14%)
  other arithmetic  34.4 us (5%)
  between operations  14.7 us (2%)
  matrix products  12.5 us (2%)
  starting transfers between devices  9.78 us (1%)
    all_gather x1, waiting for transfers between devices, local_fn(): h_all = lax.all_gather(h_loc, 'cp')  116 us
    all_gather x1, waiting for transfers between devices, local_fn(): dwq_all = lax.all_gather(dwq, 'cp').reshape(NB, 2, 2, DM, HD)  78.1 us
    all_gather x1, waiting for transfers between devices, local_fn(): dy_all = lax.all_gather(dy_loc, 'cp')  51 us
    all_to_all x1, waiting for transfers between devices, local_fn(): lax.all_to_all(jnp.concatenate([dqp, mine], axis=1), 'cp', 0, 0)  50.2 us
    ppermute x1, waiting for transfers between devices, local_fn(): tot = sum1[0] + lax.ppermute(sum1[1], 'cp', layer_perm)  45.4 us
    pallas_call x1, Pallas kernels, local_fn(): call(functools.partial(bwd_kernel, scale=scale), 'attn_bwd', (NB,), [full...  40.9 us
    all_to_all x1, waiting for transfers between devices, local_fn(): o_tok = lax.all_to_all(o, 'cp', 0, 0)  39.6 us
    pallas_call x1, Pallas kernels, local_fn(): call(functools.partial(lambda ix, *a, scale: fwd_kernel(*a, scale=scale),...  28.9 us
  transfers between devices with their start and end apart: 10, of which 8 were waited for; matrix products, arithmetic and copies ran while one was open for 11% of the time, Pallas kernels for 17%

profile of v1, /device:TPU:0, one launch (start us, length us, event | category | flops | bytes accessed | tf_op | source)
XLA Modules:
  0.0 688.0 jit_solution(1265615798340725835)
XLA Ops:
  13.9 116.1 %all-gather.11.cloned.1.call-done = bf16[64,128,1024]{2,1,0:T(8,128)(2,1)} async-done(((bf16[2,128,1024]{2,1,0:T(8,128)(2,1)}), bf16[64,128,1024]{2,1,0:T(8,128)(2,1)}) %all-gather.11.cloned.1.call-update) | async-done | bytes 16777232 | tf_op jit(solution)/shard_map/all_gather | solution.py:232
  135.6 7.8 %fusion.15 = (f32[4096,64]{1,0:T(8,128)S(1)}, f32[4096,64]{1,0:T(8,128)S(1)}, f32[4096,64]{1,0:T(8,128)S(1)}) fusion(f32[64]{0:T(128)S(1)} %multiply_power_fusion), kind=kLoop, calls=%fused_computation.41 | loop fusion | flops 524288 | bytes 3145984 | tf_op jit(solution)/shard_map/neg | solution.py:249
  146.8 18.8 %proj.1 = (bf16[4096,128]{1,0:T(8,128)(2,1)}, bf16[4096,128]{1,0:T(8,128)(2,1)}, bf16[4096,128]{1,0:T(8,128)(2,1)}, f32[4096,128]{1,0:T(8,128)}, f32[4096,128]{1,0:T(8,128)}) custom-call(s32[2]{0:T(128)} %pad_add_fusion.idx_ref.ix, bf16[32,2,128,1024]{3,2,1,0:T(8,128)(2,1)} %bitcast.171, bf16[32,2,128,1024]{3,2,1,0:T(8,128)(2,1)} %bitcast.172, ...), custom_call_target="tpu_custom_call" | custom-call | flops 3221225472 | bytes 8388608 | tf_op jit(solution)/shard_map/proj/pallas_call | solution.py:253
  165.6 28.9 %attn_fwd.1 = (bf16[32,128,128]{2,1,0:T(8,128)(2,1)}, f32[8,1,512]{2,1,0:T(1,128)}) custom-call(s32[2]{0:T(128)} %pad_add_fusion.idx_ref.ix, bf16[4096,128]{1,0:T(8,128)(2,1)} %get-tuple-element.25.a_0_.q_ref, bf16[4096,128]{1,0:T(8,128)(2,1)} %get-tuple-element.26.a_1_.k_ref, bf16[4096,128]{1,0:T(8,128)(2,1)} %get-tuple-element.27.a_2_.v_ref), custom_call_target="tpu_custom_call" | custom-call | flops 8589934592 | bytes 8388608 | tf_op jit(solution)/shard_map/attn_fwd/pallas_call | solution.py:262
  194.5 51.0 %all-gather.13.cloned.1.call-done = bf16[64,128,1024]{2,1,0:T(8,128)(2,1)} async-done(((bf16[2,128,1024]{2,1,0:T(8,128)(2,1)}), bf16[64,128,1024]{2,1,0:T(8,128)(2,1)}) %all-gather.13.cloned.1.call-update) | async-done | bytes 16777232 | tf_op jit(solution)/shard_map/all_gather | solution.py:234
  245.4 8.7 %dwo.1 = f32[128,1024]{1,0:T(8,128)} custom-call(s32[2]{0:T(128)} %pad_add_fusion.idx_ref.ix, bf16[32,128,128]{2,1,0:T(8,128)(2,1)} %get-tuple-element.28.o_ref, bf16[32,2,128,1024]{3,2,1,0:T(8,128)(2,1)} %bitcast.175), custom_call_target="tpu_custom_call" | custom-call | flops 1073741824 | bytes 8388608 | tf_op jit(solution)/shard_map/dwo/pallas_call | solution.py:276
  256.1 9.1 %dout.1.do_ref = bf16[4096,128]{1,0:T(8,128)(2,1)} custom-call(s32[2]{0:T(128)} %pad_add_fusion.idx_ref.ix, bf16[32,2,128,1024]{3,2,1,0:T(8,128)(2,1)} %bitcast.176, bf16[128,1024]{1,0:T(8,128)(2,1)} %dynamic-slice_select_fusion.wo_ref), custom_call_target="tpu_custom_call" | custom-call | flops 1073741824 | bytes 8388608 | tf_op jit(solution)/shard_map/dout/pallas_call | solution.py:271
  265.2 40.9 %attn_bwd.1 = (bf16[32,128,128]{2,1,0:T(8,128)(2,1)}, f32[2,2,2048,128]{3,2,1,0:T(8,128)}) custom-call(s32[2]{0:T(128)} %pad_add_fusion.idx_ref.ix, bf16[4096,128]{1,0:T(8,128)(2,1)} %get-tuple-element.25.a_0_.q_ref, bf16[4096,128]{1,0:T(8,128)(2,1)} %get-tuple-element.26.a_1_.k_ref, bf16[4096,128]{1,0:T(8,128)(2,1)} %get-tuple-element.27.a_2_.v_ref, ...), custom_call_target="tpu_custom_call" | custom-call | flops 21474836480 | bytes 8388608 | tf_op jit(solution)/shard_map/attn_bwd/pallas_call | solution.py:285
  308.3 3.9 collective-permute-done
  317.6 45.4 %collective-permute-done.1 = f32[2048,128]{1,0:T(8,128)S(1)} collective-permute-done((f32[2048,128]{1,0:T(8,128)}, f32[2048,128]{1,0:T(8,128)S(1)}, u32[]{:S(2)}, u32[]{:S(2)}) %collective-permute-start.1) | collective-permute-done | bytes 1048608 | tf_op jit(solution)/shard_map/ppermute | solution.py:310
  370.9 12.1 %collective-permute-done.2 = bf16[32,64,128]{2,1,0:T(8,128)(2,1)S(1)} collective-permute-done((bf16[32,64,128]{2,1,0:T(8,128)(2,1)S(1)}, bf16[32,64,128]{2,1,0:T(8,128)(2,1)S(1)}, u32[]{:S(2)}, u32[]{:S(2)}) %collective-permute-start.2) | collective-permute-done | bytes 524320 | tf_op jit(solution)/shard_map/ppermute | solution.py:317
  384.3 7.3 %dwkv.1 = f32[512,128]{1,0:T(8,128)} custom-call(s32[2]{0:T(128)} %pad_add_fusion.idx_ref.ix, bf16[32,2,128,1024]{3,2,1,0:T(8,128)(2,1)} %bitcast.173, bf16[32,128,128]{2,1,0:T(8,128)(2,1)} %pad_maximum_fusion.3.d_ref), custom_call_target="tpu_custom_call" | custom-call | flops 536870912 | bytes 8388608 | tf_op jit(solution)/shard_map/dwkv/pallas_call | solution.py:296
  391.7 8.6 %dwq.1 = f32[1024,128]{1,0:T(8,128)} custom-call(s32[2]{0:T(128)} %pad_add_fusion.idx_ref.ix, bf16[32,2,128,1024]{3,2,1,0:T(8,128)(2,1)} %bitcast.174, bf16[32,128,128]{2,1,0:T(8,128)(2,1)} %get-tuple-element.33.d_ref), custom_call_target="tpu_custom_call" | custom-call | flops 1073741824 | bytes 8388608 | tf_op jit(solution)/shard_map/dwq/pallas_call | solution.py:296
  404.4 39.6 %all-to-all-done = bf16[32,128,128]{2,1,0:T(8,128)(2,1)S(1)} async-done(((bf16[32,128,128]{2,1,0:T(8,128)(2,1)}), bf16[32,128,128]{2,1,0:T(8,128)(2,1)S(1)}, u32[]{:S(2)}, u32[]{:S(2)}) %all-to-all-start) | async-done | bytes 1048608 | tf_op jit(solution)/shard_map/all_to_all | solution.py:269
  456.8 50.2 %all-to-all-done.1 = bf16[32,192,128]{2,1,0:T(8,128)(2,1)S(1)} async-done(((bf16[32,192,128]{2,1,0:T(8,128)(2,1)}), bf16[32,192,128]{2,1,0:T(8,128)(2,1)S(1)}, u32[]{:S(2)}, u32[]{:S(2)}) %all-to-all-start.1) | async-done | bytes 1572896 | tf_op jit(solution)/shard_map/all_to_all | solution.py:320
  509.9 3.9 fusion.23
  519.5 4.0 slice_bitcast_fusion.2
  534.8 6.8 fusion.47
  541.6 78.1 %all-gather.17.cloned.1.call-done = f32[32768,128]{1,0:T(8,128)} async-done(((f32[1024,128]{1,0:T(8,128)}), f32[32768,128]{1,0:T(8,128)}) %all-gather.17.cloned.1.call-update) | async-done | bytes 16777232 | tf_op jit(solution)/shard_map/all_gather | solution.py:307
  619.8 9.9 %slice_bitcast_fusion = (f32[1024,8,2,128]{3,0,2,1:T(8,128)}, f32[1024,8,2,128]{3,0,2,1:T(8,128)S(1)}) fusion(f32[8,2,2,1024,128]{4,3,2,1,0:T(8,128)} %bitcast.180), kind=kLoop, calls=%fused_computation | loop fusion | bytes 33554432 | tf_op jit(solution)/shard_map/transpose | solution.py:344
  629.7 13.0 %copy.49 = f32[1024,8,2,128]{3,2,1,0:T(2,128)} copy(f32[1024,8,2,128]{3,0,2,1:T(8,128)S(1)} %get-tuple-element.43) | data formatting | bytes 16777216 | tf_op jit(solution)/shard_map/transpose | solution.py:343
  642.7 11.5 %reshape.176 = f32[1024,2048]{1,0:T(8,128)} reshape(f32[1024,8,2,128]{3,2,1,0:T(2,128)} %copy.49) | data formatting | bytes 16777216 | tf_op jit(solution)/shard_map/reshape | solution.py:343
  654.2 15.4 %copy.50 = f32[1024,8,2,128]{3,2,1,0:T(2,128)} copy(f32[1024,8,2,128]{3,0,2,1:T(8,128)} %get-tuple-element.42) | data formatting | bytes 16777216 | tf_op jit(solution)/shard_map/transpose | solution.py:344
  669.6 11.5 %reshape.177 = f32[1024,2048]{1,0:T(8,128)} reshape(f32[1024,8,2,128]{3,2,1,0:T(2,128)} %copy.50) | data formatting | bytes 16777216 | tf_op jit(solution)/shard_map/reshape | solution.py:344
  (118 shorter events, 70.8 us)
Async XLA Ops:
  7.2 5.9 copy-start.14
  7.2 5.9 copy-start.13
  7.2 122.8 %all-gather.11.cloned.1.call-start = ((), (), s32[]{:S(2)}) async-start(), calls=%async_computation.2 | async-start | bytes 17301504 | tf_op jit(solution)/shard_map/all_gather | solution.py:232
  12.9 121.6 %copy-start.18 = (bf16[128]{0:T(256)(128)(2,1)S(1)}, bf16[128]{0:T(256)(128)(2,1)}, u32[]{:S(2)}) copy-start(bf16[128]{0:T(256)(128)(2,1)} %param.29) | copy-start | bytes 772
  13.0 122.1 %copy-start.16 = (bf16[128]{0:T(256)(128)(2,1)S(1)}, bf16[128]{0:T(256)(128)(2,1)}, u32[]{:S(2)}) copy-start(bf16[128]{0:T(256)(128)(2,1)} %param.27) | copy-start | bytes 772
  13.0 122.1 %copy-start.17 = (bf16[128]{0:T(256)(128)(2,1)S(1)}, bf16[128]{0:T(256)(128)(2,1)}, u32[]{:S(2)}) copy-start(bf16[128]{0:T(256)(128)(2,1)} %param.28) | copy-start | bytes 772
  13.0 232.5 %all-gather.13.cloned.1.call-start = ((), (), s32[]{:S(2)}) async-start(), calls=%async_computation.3 | async-start | bytes 17301504 | tf_op jit(solution)/shard_map/all_gather | solution.py:234
  130.0 270.3 %all-gather.15.cloned.1.call-start = ((), (), s32[]{:S(2)}) async-start(), calls=%async_computation.4 | async-start | bytes 17301504 | tf_op jit(solution)/shard_map/all_gather | solution.py:282
  254.1 265.4 %all-gather.19.cloned.1.call-start = ((), (), s32[]{:S(2)}) async-start(), calls=%async_computation.6 | async-start | bytes 8650752 | tf_op jit(solution)/shard_map/all_gather | solution.py:322
  306.1 6.1 copy-start.9
  308.0 4.2 collective-permute-start
  314.8 48.3 %collective-permute-start.1 = (f32[2048,128]{1,0:T(8,128)}, f32[2048,128]{1,0:T(8,128)S(1)}, u32[]{:S(2)}, u32[]{:S(2)}) collective-permute-start(f32[2048,128]{1,0:T(8,128)} %slice_bitcast_fusion.5), channel_id=1, source_target_pairs={{0,2},{1,3},{2,0},{3,1},{4,6},{5,7},{6,4},{7,5},{8,10},{9,11},{10,... | collective-permute-start | bytes 3145736 | tf_op jit(solution)/shard_map/ppermute | solution.py:310
  369.5 13.4 %collective-permute-start.2 = (bf16[32,64,128]{2,1,0:T(8,128)(2,1)S(1)}, bf16[32,64,128]{2,1,0:T(8,128)(2,1)S(1)}, u32[]{:S(2)}, u32[]{:S(2)}) collective-permute-start(bf16[32,64,128]{2,1,0:T(8,128)(2,1)S(1)} %reverse_select_fusion), channel_id=1, source_target_pairs={{0,2},{1,3},{2,0},{3,1},{4,6},{5,7},{6,4},{7,5},{8,10},{9,11},{10,... | collective-permute-start | bytes 1572872 | tf_op jit(solution)/shard_map/ppermute | solution.py:317
  391.6 228.1 %all-gather.17.cloned.1.call-start = ((), (), s32[]{:S(2)}) async-start(), calls=%async_computation.5 | async-start | bytes 17301504 | tf_op jit(solution)/shard_map/all_gather | solution.py:307
  400.3 43.7 %all-to-all-start = ((bf16[32,128,128]{2,1,0:T(8,128)(2,1)}), bf16[32,128,128]{2,1,0:T(8,128)(2,1)S(1)}, u32[]{:S(2)}, u32[]{:S(2)}) async-start(bf16[32,128,128]{2,1,0:T(8,128)(2,1)} %get-tuple-element.28.o_ref), calls=%async_computation | async-start | bytes 2097152 | tf_op jit(solution)/shard_map/all_to_all | solution.py:269
  444.1 62.9 %all-to-all-start.1 = ((bf16[32,192,128]{2,1,0:T(8,128)(2,1)}), bf16[32,192,128]{2,1,0:T(8,128)(2,1)S(1)}, u32[]{:S(2)}, u32[]{:S(2)}) async-start(bf16[32,192,128]{2,1,0:T(8,128)(2,1)} %pad_maximum_fusion.2), calls=%async_computation.1 | async-start | bytes 3145728 | tf_op jit(solution)/shard_map/all_to_all | solution.py:320
  447.8 3.7 copy-start.4
  451.5 3.8 copy-start.5
  451.5 3.8 copy-start.6
  509.9 4.0 copy-start.11
  509.9 4.8 copy-start.12
  523.6 11.3 %slice-start = ((s8[16777216]{0:T(1024)(128)(4,1)}), s8[4194304]{0:T(1024)(128)(4,1)S(1)}, s32[]{:S(2)}) async-start(s8[16777216]{0:T(1024)(128)(4,1)} %bitcast.177), calls=%async_computation.7 | async-start | bytes 8388608
  526.0 8.8 %slice-start.1 = ((s8[16777216]{0:T(1024)(128)(4,1)}), s8[4194304]{0:T(1024)(128)(4,1)S(1)}, s32[]{:S(2)}) async-start(s8[16777216]{0:T(1024)(128)(4,1)} %bitcast.177), calls=%async_computation.8 | async-start | bytes 8388608
  529.1 5.8 slice-start.2
  (9 other events, 22.5 us)
Sparse Core Ops, SparseCore 0:
  13.1 116.8 all-gather.10
  132.9 112.5 all-gather.12
  254.2 134.6 all-gather.14
  392.2 110.8 all-gather.18
  506.4 113.3 all-gather.16
